TPU v7x, 32 devices: a whole 2x2x4 slice. The times are simulated.
32 devices in a mesh: grp: 4 (over z), dev: 8 (over y, x, core).
Axes of the slice: x: 2, y: 2, z: 4, core: 2. Of those that a mesh axis runs over, the one named last changes fastest.
Arguments:
- qkv_weight: bfloat16 [2, 4608, 8192], P(None, ('grp', 'dev')), may hold values from -0.09375 to 0.09375
- gate_up_weight: bfloat16 [2, 4608, 73728], P(None, ('grp', 'dev')), may hold values from -0.09375 to 0.09375
- head_slot: int32 [64], replicated, may hold values from 0 to 63, each once
- layer_ids: int32 [2], replicated, may hold values from 0 to 45
- stored_qkv: int32 [46, 64], replicated, may hold values from -16384 to 16383
- stored_gate_up: int32 [46, 576], replicated, may hold values from -16384 to 16383
Outputs:
- served_qkv: bfloat16 [2, 4608, 8192], P(None, 'grp', 'dev')
- served_gate_up: bfloat16 [2, 4608, 73728], P(None, 'grp', 'dev')
- qkv_mismatch: float32 [2, 64], P(None, 'dev')
- gate_up_mismatch: float32 [2, 576], P(None, 'dev')
Inputs may be any that keep to these rules, and one draw needn't show every extreme that they name: `head_slot`: each of the 64 heads appears once.
All inputs are finite; a program needn't handle non-finite values.
Results may differ from a plain program's by a relative error of at most 0.0004.
Values may be sent and summed in bfloat16 or wider, within the bound.
A program may use at most 256 MiB of HBM per device.

v0:
```python
import jax
import jax.numpy as jnp
from jax import lax
from jax.sharding import PartitionSpec as P

HEAD_DIM = 128
FF = 36864
STORED = 46
BLK = 128
NHEAD = 64
stored_unit = 1.0 / 1024.0


def finish(pieces):
    qkv_piece, gate_piece = pieces
    count = qkv_piece.shape[0]
    height = qkv_piece.shape[1]
    served_qkv = qkv_piece.reshape(count, height, qkv_piece.shape[4])
    served_gate = gate_piece.reshape(count, height, 2 * gate_piece.shape[4])
    return (served_qkv, served_gate)


def body(qkv_weight, gate_up_weight, head_slot, layer_ids, stored_qkv, stored_gate_up):
    owners = lax.axis_size("dev")
    owner = lax.axis_index("dev")
    layers = qkv_weight.shape[0]
    rows = qkv_weight.shape[1]
    slots = NHEAD // owners
    width = FF // owners
    blocks = width // BLK
    ordered = qkv_weight.reshape(layers, rows, NHEAD, HEAD_DIM)[:, :, head_slot, :]
    qkv_split = ordered.reshape(layers, rows, 1, owners, slots * HEAD_DIM)
    gate_split = gate_up_weight.reshape(layers, rows, 2, owners, width)
    moved = (
        lax.all_to_all(qkv_split, "dev", split_axis=3, concat_axis=1, tiled=True),
        lax.all_to_all(gate_split, "dev", split_axis=3, concat_axis=1, tiled=True),
    )
    results = finish(moved)
    served_qkv = results[0]
    served_gate = results[1]
    head_part = jnp.sum(ordered.astype(jnp.float32), axis=(1, 3))
    block_part = jnp.sum(
        gate_split.astype(jnp.float32).reshape(layers, rows, 2, owners, blocks, BLK), axis=(1, 5)
    )
    block_part = block_part.transpose(0, 2, 1, 3).reshape(layers, owners * 2 * blocks)
    head_all, block_all = lax.psum((head_part, block_part), ("grp", "dev"))
    head_sum = lax.dynamic_slice_in_dim(head_all, owner * slots, slots, 1)
    block_sum = lax.dynamic_slice_in_dim(block_all, owner * 2 * blocks, 2 * blocks, 1)
    layer_pick = (layer_ids[:, None] == jnp.arange(STORED, dtype=jnp.int32)[None, :]).astype(
        jnp.float32
    )
    picked_qkv = jnp.dot(
        layer_pick,
        stored_qkv.astype(jnp.float32),
        precision=lax.Precision.HIGHEST,
        preferred_element_type=jnp.float32,
    )
    picked_gate = jnp.dot(
        layer_pick,
        stored_gate_up.astype(jnp.float32),
        precision=lax.Precision.HIGHEST,
        preferred_element_type=jnp.float32,
    )
    own_heads = lax.dynamic_slice_in_dim(head_slot, owner * slots, slots, 0)
    picked_qkv = picked_qkv[:, own_heads]
    picked_gate = (
        picked_gate.reshape(layers, 2, owners, blocks)
        .transpose(0, 2, 1, 3)
        .reshape(layers, owners * 2 * blocks)
    )
    picked_gate = lax.dynamic_slice_in_dim(picked_gate, owner * 2 * blocks, 2 * blocks, 1)
    qkv_mismatch = head_sum - picked_qkv * stored_unit
    gate_up_mismatch = block_sum - picked_gate * stored_unit
    return (served_qkv, served_gate, qkv_mismatch, gate_up_mismatch)


def solution(mesh):
    placed = (P(None, ("grp", "dev"), None), P(None, ("grp", "dev"), None), P(), P(), P(), P())
    return jax.shard_map(
        body,
        mesh=mesh,
        in_specs=placed,
        out_specs=(P(None, "grp", "dev"), P(None, "grp", "dev"), P(None, "dev"), P(None, "dev")),
        check_vma=False,
    )
```

profile of v0, /device:TPU:0, one launch (start us, length us, event | category | flops | bytes accessed | tf_op | source)
XLA Modules:
  0.0 738.6 jit_solution(3566983164668967660)
XLA Ops:
  0.6 0.7 compare_select_fusion.1
  1.3 5.3 copy_bitcast_fusion
  6.6 5.7 gather_fusion
  12.3 6.3 copy.34
  18.6 8.2 %reshape.39 = bf16[2,144,1,8,1024]{4,3,1,0,2:T(8,128)(2,1)} reshape(bf16[2,144,64,128]{3,2,1,0:T(8,128)(2,1)} %copy.34) | data formatting | bytes 9437184 | tf_op jit(solution)/shard_map/reshape | solution.py:32
  26.8 7.1 copy.35
  33.9 5.2 all-to-all-start
  39.1 29.1 %copy.45 = bf16[36,8,16,4608]{3,2,1,0:T(8,128)(2,1)} copy(bf16[36,8,16,4608]{3,1,2,0:T(8,128)(2,1)} %bitcast.27) | data formatting | bytes 84934656
  68.2 59.8 %copy.37 = bf16[2,144,2,8,4608]{4,2,1,0,3:T(2,128)(2,1)} copy(bf16[2,144,2,8,4608]{4,3,2,1,0:T(8,128)(2,1)} %bitcast.28) | data formatting | bytes 84934656 | tf_op jit(solution)/shard_map/reshape | solution.py:33
  128.0 0.0 copy-start
  128.0 0.0 copy-start.1
  128.0 0.0 all-to-all-done
  128.1 8.2 %all-to-all-start.1 = ((bf16[2,144,2,8,4608]{4,2,1,0,3:T(2,128)(2,1)}), bf16[2,144,2,8,4608]{4,2,1,0,3:T(2,128)(2,1)}, u32[]{:S(2)}, u32[]{:S(2)}) async-start(bf16[2,144,2,8,4608]{4,2,1,0,3:T(2,128)(2,1)} %copy.37), calls=%async_computation.1 | async-start | bytes 84934656 | tf_op jit(solution)/shard_map/all_to_all | solution.py:36
  136.2 0.0 copy-done
  136.2 0.0 copy-done.1
  136.2 0.2 fusion
  136.4 0.1 reshape.44
  136.6 0.1 reshape.45
  136.7 0.0 copy-start.3
  136.7 0.0 copy-start.2
  136.7 14.8 %convert_reduce_fusion = f32[2,73728]{1,0:T(2,128)S(1)} fusion(bf16[2,144,73728]{2,1,0:T(8,128)(2,1)} %param.7), kind=kLoop, calls=%fused_computation.2 | loop fusion | flops 42319872 | bytes 43057152 | tf_op jit(solution)/shard_map/reduce_sum | solution.py:42
  151.5 0.5 reduce_sum.27
  152.0 0.2 reduce_sum.28
  152.2 0.1 reshape.43
  152.3 0.0 copy-done.3
  152.4 0.1 compare_select_fusion
  152.4 0.0 copy-done.2
  152.4 0.2 fusion.2
  152.7 0.6 gather_fusion.1
  153.2 3.1 convert_reduce_fusion.1
  156.4 473.4 %all-reduce = (f32[2,64]{0,1:T(8,128)S(1)}, f32[2,576]{1,0:T(2,128)S(1)}) all-reduce(f32[2,64]{0,1:T(8,128)S(1)} %convert_reduce_fusion.1, f32[2,576]{1,0:T(2,128)S(1)} %reshape.43), channel_id=1, replica_groups=mesh['grp'=4,'dev'=8] {'grp','dev'}, use_global_device_ids=true, to_apply=%region_1.0 | all-reduce | flops 1280 | bytes 10240 | tf_op jit(solution)/shard_map/psum | solution.py:46
  629.8 0.6 copy.42
  630.4 0.6 multiply_subtract_fusion
  631.1 5.2 copy.36
  636.3 0.0 all-to-all-done.1
  636.3 36.7 %copy.38 = bf16[2,8,144,2,1,4608]{5,3,2,1,0,4:T(2,128)(2,1)} copy(bf16[2,8,144,2,1,4608]{5,3,2,0,1,4:T(2,128)(2,1)} %bitcast.5) | data formatting | bytes 84934656 | tf_op jit(solution)/shard_map/all_to_all | solution.py:36
  673.0 65.6 %reshape.42 = bf16[2,1152,9216]{2,1,0:T(8,128)(2,1)} reshape(bf16[2,8,144,2,1,4608]{5,3,2,1,0,4:T(2,128)(2,1)} %copy.38) | data formatting | bytes 84934656 | tf_op jit(solution)/shard_map/reshape | solution.py:19
  (5 shorter events, 0.0 us)
Async XLA Ops:
  33.9 94.1 %all-to-all-start = ((bf16[2,144,1,8,1024]{4,1,0,2,3:T(8,128)(2,1)}), bf16[2,144,1,8,1024]{4,1,0,2,3:T(8,128)(2,1)}, u32[]{:S(2)}, u32[]{:S(2)}) async-start(bf16[2,144,1,8,1024]{4,1,0,2,3:T(8,128)(2,1)} %copy.35), calls=%async_computation | async-start | bytes 9437184 | tf_op jit(solution)/shard_map/all_to_all | solution.py:35
  128.0 8.2 %copy-start = (s32[46,576]{1,0:T(8,128)S(1)}, s32[46,576]{1,0:T(8,128)}, u32[]{:S(2)}) copy-start(s32[46,576]{1,0:T(8,128)} %param.11) | copy-start | bytes 317956
  128.0 8.2 %copy-start.1 = (s32[2]{0:T(128)S(1)}, s32[2]{0:T(128)}, u32[]{:S(2)}) copy-start(s32[2]{0:T(128)} %param.9) | copy-start | bytes 28
  128.1 508.3 %all-to-all-start.1 = ((bf16[2,144,2,8,4608]{4,2,1,0,3:T(2,128)(2,1)}), bf16[2,144,2,8,4608]{4,2,1,0,3:T(2,128)(2,1)}, u32[]{:S(2)}, u32[]{:S(2)}) async-start(bf16[2,144,2,8,4608]{4,2,1,0,3:T(2,128)(2,1)} %copy.37), calls=%async_computation.1 | async-start | bytes 84934656 | tf_op jit(solution)/shard_map/all_to_all | solution.py:36
  136.7 15.7 %copy-start.3 = (s32[64]{0:T(128)S(1)}, s32[64]{0:T(128)}, u32[]{:S(2)}) copy-start(s32[64]{0:T(128)} %param.8) | copy-start | bytes 772
  136.7 15.8 %copy-start.2 = (s32[46,64]{1,0:T(8,128)S(1)}, s32[46,64]{1,0:T(8,128)}, u32[]{:S(2)}) copy-start(s32[46,64]{1,0:T(8,128)} %param.10) | copy-start | bytes 35332
where the time goes:
time: 741 us; the launch traced here: 739 us
  blocking collectives  473 us (64%)
  local copies, waits for them, and re-layouts  231 us (31%)
  other arithmetic  19.6 us (3%)
  starting transfers between devices  13.4 us (2%)
    psum x1, blocking collectives, body(): head_all, block_all = lax.psum((head_part, block_part), ('grp', 'dev'))  473 us
    reshape x1, local copies, waits for them, and re-layouts, finish(): served_gate = gate_piece.reshape(count, height, 2 * gate_piece.shape[4])  65.6 us
    reshape x1, local copies, waits for them, and re-layouts, body(): gate_split = gate_up_weight.reshape(layers, rows, 2, owners, width)  59.8 us
    all_to_all x1, local copies, waits for them, and re-layouts, body(): lax.all_to_all(gate_split, 'dev', split_axis=3, concat_axis=1, tiled=True)  36.7 us
    unnamed x10, local copies, waits for them, and re-layouts  29.7 us
    reshape x2, local copies, waits for them, and re-layouts, body(): qkv_split = ordered.reshape(layers, rows, 1, owners, slots * HEAD_DIM)  15.3 us
    reduce_sum x2, other arithmetic, body(): jnp.sum(gate_split.astype(jnp.float32).reshape(layers, rows, 2, owners, b...  15 us
  transfers between devices with their start and end apart: 2, of which 0 were waited for; matrix products, arithmetic and copies ran while one was open for 16% of the time, Pallas kernels for 0%

commit v1 on v0

--- a/solution.py
+++ b/solution.py
@@ -9,6 +9,13 @@
 BLK = 128
 NHEAD = 64
 stored_unit = 1.0 / 1024.0
+
+
+def swap_blocks(x, name, split, join):
+    size = lax.axis_size(name)
+    pieces = jnp.stack(jnp.split(x, size, axis=split), axis=0)
+    pieces = lax.all_to_all(pieces, name, split_axis=0, concat_axis=0)
+    return jnp.concatenate(pieces, axis=join)
 
 
 def finish(pieces):
@@ -33,7 +40,7 @@
     gate_split = gate_up_weight.reshape(layers, rows, 2, owners, width)
     moved = (
         lax.all_to_all(qkv_split, "dev", split_axis=3, concat_axis=1, tiled=True),
-        lax.all_to_all(gate_split, "dev", split_axis=3, concat_axis=1, tiled=True),
+        swap_blocks(gate_split, "dev", 3, 1),
     )
     results = finish(moved)
     served_qkv = results[0]

time: 741 us -> 955 us (1.29)
  local copies, waits for them, and re-layouts: 231 us -> 444 us
    another operation x0 -> x3, local copies, waits for them, and re-layouts: none -> 146 us  [the longest x2 80.4 us: swap_blocks(): pieces = jnp.stack(jnp.split(x, size, axis=split), axis=0)]
    split x0 -> x1, local copies, waits for them, and re-layouts: none -> 137 us  [swap_blocks(): pieces = jnp.stack(jnp.split(x, size, axis=split), axis=0)]
    reshape x2 -> x1, local copies, waits for them, and re-layouts: 125 us -> 36.7 us  [swap_blocks(): return jnp.concatenate(pieces, axis=join)]
    unnamed x10 -> x17, local copies, waits for them, and re-layouts: 29.7 us -> 85.4 us
    all_to_all x1 -> x0, local copies, waits for them, and re-layouts: 36.7 us -> none  [body(): lax.all_to_all(gate_split, 'dev', split_axis=3, concat_axis=1, tiled=True)]
  transfers between devices with their start and end apart: 2 -> 2, of which waited for: 0 -> 0; matrix products, arithmetic and copies ran while one was open for 16% -> 35% of each run, Pallas kernels for 0% -> 0%
where the time goes in v1:
time: 955 us; the launch traced here: 952 us
  blocking collectives  474 us (50%)
  local copies, waits for them, and re-layouts  444 us (46%)
  other arithmetic  19.6 us (2%)
  starting transfers between devices  13 us (1%)
    psum x1, blocking collectives, body(): head_all, block_all = lax.psum((head_part, block_part), ('grp', 'dev'))  474 us
    split x1, local copies, waits for them, and re-layouts, swap_blocks(): pieces = jnp.stack(jnp.split(x, size, axis=split), axis=0)  137 us
    unnamed x17, local copies, waits for them, and re-layouts  85.4 us
    another operation x2, local copies, waits for them, and re-layouts, swap_blocks(): pieces = jnp.stack(jnp.split(x, size, axis=split), axis=0)  80.4 us
    another operation x1, local copies, waits for them, and re-layouts, finish(): served_gate = gate_piece.reshape(count, height, 2 * gate_piece.shape[4])  65.6 us
    reshape x1, local copies, waits for them, and re-layouts, swap_blocks(): return jnp.concatenate(pieces, axis=join)  36.7 us
  transfers between devices with their start and end apart: 2, of which 0 were waited for; matrix products, arithmetic and copies ran while one was open for 35% of the time, Pallas kernels for 0%

profile of v1, /device:TPU:0, one launch (start us, length us, event | category | flops | bytes accessed | tf_op | source)
XLA Modules:
  0.0 951.9 jit_solution(13559149965136919080)
XLA Ops:
  0.6 5.3 copy_bitcast_fusion
  6.0 0.7 compare_select_fusion.1
  6.6 5.7 gather_fusion
  12.3 6.3 copy.211
  18.6 8.2 reshape.38
  26.8 7.1 copy.212
  33.9 5.2 all-to-all-start
  39.1 29.1 %copy.230 = bf16[36,8,16,4608]{3,2,1,0:T(8,128)(2,1)} copy(bf16[36,8,16,4608]{3,1,2,0:T(8,128)(2,1)} %bitcast.42) | data formatting | bytes 84934656
  68.2 136.7 %fusion.6 = (bf16[2,144,2,1,4608]{4,3,2,1,0:T(2,128)(2,1)S(1)}, bf16[2,144,2,1,4608]{4,3,2,1,0:T(2,128)(2,1)}, bf16[2,144,2,1,4608]{4,3,2,1,0:T(2,128)(2,1)}, bf...) fusion(bf16[2,144,2,8,4608]{4,3,2,1,0:T(8,128)(2,1)} %bitcast.41), kind=kLoop, calls=%fused_computation.26 | loop fusion | bytes 84934656 | tf_op jit(solution)/shard_map/split | solution.py:16
  205.0 8.0 bitcast_dynamic-update-slice_fusion.7
  212.9 8.0 bitcast_dynamic-update-slice_fusion.6
  220.9 8.0 bitcast_dynamic-update-slice_fusion.5
  228.8 8.0 bitcast_dynamic-update-slice_fusion.4
  236.8 8.0 bitcast_dynamic-update-slice_fusion.3
  244.7 8.0 bitcast_dynamic-update-slice_fusion.2
  252.7 8.0 bitcast_dynamic-update-slice_fusion.1
  260.6 4.2 bitcast_dynamic-update-slice_fusion
  264.8 76.2 %copy.222 = bf16[8,2,144,2,1,4608]{5,3,2,1,4,0:T(2,128)(2,1)} copy(bf16[8,2,144,2,1,4608]{5,2,4,3,1,0:T(8,128)(2,1)} %bitcast_dynamic-update-slice_fusion) | data formatting | bytes 84934656 | tf_op jit(solution)/shard_map/stack | solution.py:16
  341.0 0.0 all-to-all-done
  341.0 7.8 all-to-all-start.1
  348.9 0.0 copy-start.3
  348.9 0.0 copy-start.1
  348.9 0.0 copy-start.2
  348.9 0.0 copy-start
  348.9 14.8 %convert_reduce_fusion = f32[2,73728]{1,0:T(2,128)S(1)} fusion(bf16[2,144,73728]{2,1,0:T(8,128)(2,1)} %param.7), kind=kLoop, calls=%fused_computation.2 | loop fusion | flops 42319872 | bytes 43057152 | tf_op jit(solution)/shard_map/reduce_sum | solution.py:49
  363.7 0.5 reduce_sum.27
  364.2 0.2 reduce_sum.28
  364.5 0.1 reshape.42
  364.6 0.0 copy-done.3
  364.6 0.1 compare_select_fusion
  364.7 0.0 copy-done.1
  364.7 0.0 copy-done.2
  364.7 0.2 fusion.2
  364.9 0.6 gather_fusion.1
  365.5 3.1 convert_reduce_fusion.1
  368.6 474.0 %all-reduce = (f32[2,64]{0,1:T(8,128)S(1)}, f32[2,576]{1,0:T(2,128)S(1)}) all-reduce(f32[2,64]{0,1:T(8,128)S(1)} %convert_reduce_fusion.1, f32[2,576]{1,0:T(2,128)S(1)} %reshape.42), channel_id=1, replica_groups=mesh['grp'=4,'dev'=8] {'grp','dev'}, use_global_device_ids=true, to_apply=%region_1.0 | all-reduce | flops 1280 | bytes 10240 | tf_op jit(solution)/shard_map/psum | solution.py:53
  842.6 0.6 copy.227
  843.3 0.0 copy-done
  843.3 0.2 fusion
  843.5 0.1 reshape.43
  843.6 0.1 reshape.44
  843.7 0.6 multiply_subtract_fusion
  844.3 5.2 copy.213
  849.6 0.0 all-to-all-done.1
  849.6 36.7 %copy.223 = bf16[2,8,144,2,1,4608]{5,3,2,1,0,4:T(2,128)(2,1)} copy(bf16[2,8,144,2,1,4608]{5,3,2,0,4,1:T(2,128)(2,1)} %bitcast.12) | data formatting | bytes 84934656 | tf_op jit(solution)/shard_map/reshape | solution.py:18
  886.3 65.6 %reshape_reshape.3 = bf16[2,1152,9216]{2,1,0:T(8,128)(2,1)} reshape(bf16[2,8,144,2,1,4608]{5,3,2,1,0,4:T(2,128)(2,1)} %copy.223) | data formatting | bytes 84934656 | tf_op jit(solution)/shard_map/reshape;reshape | solution.py:26
  (5 shorter events, 0.0 us)
Async XLA Ops:
  33.9 307.1 %all-to-all-start = ((bf16[2,144,1,8,1024]{4,1,0,2,3:T(8,128)(2,1)}), bf16[2,144,1,8,1024]{4,1,0,2,3:T(8,128)(2,1)}, u32[]{:S(2)}, u32[]{:S(2)}) async-start(bf16[2,144,1,8,1024]{4,1,0,2,3:T(8,128)(2,1)} %copy.212), calls=%async_computation | async-start | bytes 9437184 | tf_op jit(solution)/shard_map/all_to_all | solution.py:42
  341.0 508.5 %all-to-all-start.1 = ((bf16[8,2,144,2,1,4608]{5,3,2,1,4,0:T(2,128)(2,1)}), bf16[8,2,144,2,1,4608]{5,3,2,1,4,0:T(2,128)(2,1)}, u32[]{:S(2)}, u32[]{:S(2)}) async-start(bf16[8,2,144,2,1,4608]{5,3,2,1,4,0:T(2,128)(2,1)} %copy.222), calls=%async_computation.1 | async-start | bytes 84934656 | tf_op jit(solution)/shard_map/all_to_all | solution.py:17
  348.9 15.7 %copy-start.3 = (s32[64]{0:T(128)S(1)}, s32[64]{0:T(128)}, u32[]{:S(2)}) copy-start(s32[64]{0:T(128)} %param.8) | copy-start | bytes 772
  348.9 15.8 %copy-start.1 = (s32[2]{0:T(128)S(1)}, s32[2]{0:T(128)}, u32[]{:S(2)}) copy-start(s32[2]{0:T(128)} %param.9) | copy-start | bytes 28
  348.9 15.8 %copy-start.2 = (s32[46,64]{1,0:T(8,128)S(1)}, s32[46,64]{1,0:T(8,128)}, u32[]{:S(2)}) copy-start(s32[46,64]{1,0:T(8,128)} %param.10) | copy-start | bytes 35332
  348.9 494.3 %copy-start = (s32[46,576]{1,0:T(8,128)S(1)}, s32[46,576]{1,0:T(8,128)}, u32[]{:S(2)}) copy-start(s32[46,576]{1,0:T(8,128)} %param.11) | copy-start | bytes 317956
